TPU v7x, 32 devices: a whole 2x2x4 slice. The times are simulated.
32 devices in a mesh: dp: 2 (over x), rep: 4 (over y, core), ind: 4 (over z).
Axes of the slice: x: 2, y: 2, z: 4, core: 2. Of those that a mesh axis runs over, the one named last changes fastest.
Arguments:
- points: bfloat16 [6144, 64], P(('dp', 'rep')), may hold values from -6 to 6
- targets: float32 [6144], P(('dp', 'rep')), may hold values from -6 to 6
- inducing: float32 [4096, 64], P('ind'), may hold values from -6 to 6
- whitening: bfloat16 [4096, 4096], P('ind'), may hold values from -0.0546875 to 0.0546875
- mean_v: float32 [4096], P('ind'), may hold values from -12 to 12
- covariance: float32 [4096, 4096], P('ind', ('dp', 'rep')), may hold values from -24 to 24
- precision: float32 [4096, 4096], P('ind', ('dp', 'rep')), may hold values from -3 to 3
- natural_one: float32 [4096], P('ind'), may hold values from -6 to 6
- lengthscales: float32 [64], replicated, may hold values from 1.6 to 24
- hypers: float32 [2], replicated, may hold values from 0.5 to 2
Outputs:
- precision_new: float32 [4096, 4096], P('ind', ('dp', 'rep'))
- natural_new: float32 [4096], P('ind')
- expected_fit: float32 [], replicated
All inputs are finite; a program needn't handle non-finite values.
Results may differ from a plain program's by a relative error of at most 0.0076.
Values may be sent and summed in bfloat16 or wider, within the bound.
A program may use at most 128 MiB of HBM per device.

v0:
```python
import jax
import jax.numpy as jnp
from jax import lax
from jax.sharding import PartitionSpec as P


def cross_cov(inducing, points, lengthscales, signal):
    scaled_z = inducing / lengthscales
    scaled_x = points.astype(jnp.float32) / lengthscales
    norm_z = jnp.sum(scaled_z * scaled_z, axis=1)
    norm_x = jnp.sum(scaled_x * scaled_x, axis=1)
    inner = jnp.dot(scaled_z, scaled_x.T, precision=lax.Precision.HIGHEST)
    return (signal * jnp.exp(-0.5 * (norm_z[:, None] + norm_x[None, :] - 2.0 * inner))).astype(
        jnp.bfloat16
    )


def shards(
    points,
    targets,
    inducing,
    whitening,
    mean_v,
    covariance,
    precision,
    natural_one,
    lengthscales,
    hypers,
):
    signal = hypers[0]
    noise_var = hypers[1]
    all_inducing = lax.all_gather(inducing, "ind", axis=0, tiled=True)
    cross = cross_cov(all_inducing, points, lengthscales, signal)
    white = jnp.dot(whitening, cross, preferred_element_type=jnp.float32).astype(jnp.bfloat16)
    white_wide = white.astype(jnp.float32)
    mean_part = jnp.dot(mean_v, white_wide, precision=lax.Precision.HIGHEST)
    square_part = jnp.sum(white_wide * white_wide, axis=0)
    gram_part = lax.dot_general(
        white,
        lax.all_gather(white, "ind", axis=0, tiled=True),
        (((1,), (1,)), ((), ())),
        preferred_element_type=jnp.float32,
    )
    pred_mean, sq_norm = lax.psum((mean_part, square_part), "ind")
    resid = targets - pred_mean
    local_fit = jnp.sum(resid * resid + signal - sq_norm)
    local_proj = jnp.dot(white_wide, targets, precision=lax.Precision.HIGHEST)
    proj, fit_sum = lax.psum((local_proj, local_fit), ("dp", "rep"))
    own_rows = gram_part.shape[0]
    gram = lax.psum_scatter(gram_part, ("dp", "rep"), scatter_dimension=1, tiled=True)
    own_cols = gram.shape[1]
    trace = lax.psum(jnp.sum(covariance * gram), ("dp", "rep", "ind"))
    total = points.shape[0] * lax.axis_size(("dp", "rep"))
    expected_fit = -0.5 * jnp.log(2.0 * jnp.pi * noise_var) - (fit_sum + trace) / (
        2.0 * noise_var * total
    )
    row_ids = lax.axis_index("ind") * own_rows + jnp.arange(own_rows, dtype=jnp.int32)
    col_ids = lax.axis_index(("dp", "rep")) * own_cols + jnp.arange(own_cols, dtype=jnp.int32)
    identity = (row_ids[:, None] == col_ids[None, :]).astype(jnp.float32)
    precision_new = 0.5 * precision + 0.5 * (identity + gram / noise_var)
    natural_new = 0.5 * natural_one + 0.5 * proj / noise_var
    return (precision_new, natural_new, expected_fit)


def solution(mesh):
    return jax.shard_map(
        shards,
        mesh=mesh,
        in_specs=(
            P(("dp", "rep"), None),
            P(("dp", "rep")),
            P("ind", None),
            P("ind", None),
            P("ind"),
            P("ind", ("dp", "rep")),
            P("ind", ("dp", "rep")),
            P("ind"),
            P(),
            P(),
        ),
        out_specs=(P("ind", ("dp", "rep")), P("ind"), P()),
        check_vma=False,
    )
```

profile of v0, /device:TPU:0, one launch (start us, length us, event | category | flops | bytes accessed | tf_op | source)
XLA Modules:
  0.0 361.2 jit_solution(7977664895981380709)
XLA Ops:
  7.2 0.0 copy-start
  7.2 0.0 all-gather.3.cloned.1.call-start
  7.2 0.7 all-gather.3.cloned.1.call-update
  7.9 0.0 all-gather.5.cloned.1.call-start
  8.0 1.3 fusion.4
  9.3 1.0 multiply_reduce_fusion.3
  10.3 30.0 %all-gather.3.cloned.1.call-done = f32[4096,64]{0,1:T(8,128)} async-done(((f32[1024,64]{0,1:T(8,128)}), f32[4096,64]{0,1:T(8,128)}) %all-gather.3.cloned.1.call-update) | async-done | bytes 1048592 | tf_op jit(solution)/shard_map/all_gather | solution.py:32
  40.3 0.0 slice-start
  40.3 1.6 multiply_reduce_fusion.2
  41.9 0.0 slice-start.1
  41.9 14.8 %multiply_convert_fusion = bf16[4096,768]{1,0:T(8,128)(2,1)S(1)} fusion(f32[768]{0:T(1024)S(1)} %multiply_reduce_fusion.3, f32[4096]{0:T(1024)S(1)} %multiply_reduce_fusion.2, f32[]{:T(128)} %bitcast, f32[4096,64]{0,1:T(8,128)} %all-gather.3.cloned.1.call-done, f32[64]{0:T(128)} %param.18, bf16[768,64]{0,1:T(8,128)(2,1)} %param.10), kind=kOutput, calls=%fused_computation | convolution fusion | flops 2435153920 | bytes 7458052 | tf_op jit(solution)/shard_map/dot_general | solution.py:12
  56.7 0.0 slice-done
  56.7 0.0 slice-done.1
  56.7 7.9 %multiply_reduce_fusion = (f32[768]{0:T(1024)S(1)}, bf16[768,1024]{1,0:T(8,128)(2,1)}) fusion(bf16[4096,768]{1,0:T(8,128)(2,1)S(1)} %multiply_convert_fusion, bf16[1024,4096]{1,0:T(8,128)(2,1)S(1)} %bitcast.20), kind=kOutput, calls=%fused_computation.1 | convolution fusion | flops 6445595648 | bytes 16256000 | tf_op jit(solution)/shard_map/dot_general | solution.py:34
  64.6 0.0 all-gather.5.cloned.1.call-update
  64.6 0.2 reduce-scatter.2.cloned.1.call-start
  64.8 114.6 %all-gather.5.cloned.1.call-done = bf16[4096,768]{0,1:T(8,128)(2,1)} async-done(((bf16[1024,768]{0,1:T(8,128)(2,1)}), bf16[4096,768]{0,1:T(8,128)(2,1)}) %all-gather.5.cloned.1.call-update) | async-done | bytes 6291472 | tf_op jit(solution)/shard_map/all_gather | solution.py:40
  179.5 12.5 %fusion.5 = f32[1024,4096]{1,0:T(8,128)} fusion(bf16[768,1024]{1,0:T(8,128)(2,1)} %get-tuple-element.12, bf16[4096,768]{0,1:T(8,128)(2,1)} %all-gather.5.cloned.1.call-done), kind=kOutput, calls=%fused_computation.19 | convolution fusion | flops 6442450944 | bytes 24641536 | tf_op jit(solution)/shard_map/dot_general | solution.py:38
  192.0 0.0 copy-start.2
  192.0 0.0 copy-start.1
  192.0 0.0 reduce-scatter.2.cloned.1.call-update
  192.0 0.0 copy-start.3
  192.1 0.6 copy-done.2
  194.1 0.0 copy-done
  194.1 0.0 copy-done.1
  194.1 1.3 convolution_reduce_fusion
  195.4 8.8 %all-reduce.1 = (f32[768]{0:T(1024)S(1)}, f32[768]{0:T(1024)S(1)}) all-reduce(f32[768]{0:T(1024)S(1)} %get-tuple-element.11, f32[768]{0:T(1024)S(1)} %convolution_reduce_fusion), channel_id=1, replica_groups=mesh['dp'=2,'rep'=4,'ind'=4] {'ind'}, use_global_device_ids=true, to_apply=%region_6.0 | all-reduce | flops 1536 | bytes 12288 | tf_op jit(solution)/shard_map/psum | solution.py:44
  204.2 1.3 subtract_reduce_fusion
  205.5 0.7 fusion.2
  206.2 12.9 %all-reduce = (f32[1024]{0:T(1024)S(1)}, f32[]{:T(128)}) all-reduce(f32[1024]{0:T(1024)S(1)} %bitcast.18, f32[]{:T(128)} %subtract_reduce_fusion), channel_id=1, replica_groups=mesh['dp'=2,'rep'=4,'ind'=4] {'dp','rep'}, use_global_device_ids=true, to_apply=%region_3.0 | all-reduce | flops 1025 | bytes 8200 | tf_op jit(solution)/shard_map/psum | solution.py:48
  219.2 0.0 copy-done.3
  219.2 1.2 divide_add_fusion
  220.4 86.0 %reduce-scatter.2.cloned.1.call-done = f32[1024,512]{1,0:T(8,128)} async-done(((f32[1024,4096]{1,0:T(8,128)}), f32[1024,512]{1,0:T(8,128)}) %reduce-scatter.2.cloned.1.call-update) | async-done | bytes 2097168 | tf_op jit(solution)/shard_map/reduce_scatter | solution.py:50
  306.4 6.4 %multiply_reduce_fusion.1 = (f32[]{:T(128)}, f32[1024,512]{1,0:T(8,128)}) fusion(f32[1024,512]{1,0:T(8,128)} %param.15, f32[1024,512]{1,0:T(8,128)} %reduce-scatter.2.cloned.1.call-done, f32[1024,512]{1,0:T(8,128)} %param.16, f32[]{:T(128)} %bitcast.2, s32[512]{0:T(512)S(1)} %iota_add_fusion.1, s32[1024]{0:T(1024)S(1)} %iota_add_fusion), kind=kLoop, calls=%fused_computation.2 | loop fusion | flops 4194303 | bytes 8394760 | tf_op jit(solution)/shard_map/reduce_sum | solution.py:52
  312.8 39.5 %psum.39 = f32[]{:T(128)} all-reduce(f32[]{:T(128)} %get-tuple-element.7), channel_id=1, replica_groups=mesh['dp'=2,'rep'=4,'ind'=4] {'dp','rep','ind'}, use_global_device_ids=true, to_apply=%region_10.0 | all-reduce | flops 1 | bytes 8 | tf_op jit(solution)/shard_map/psum | solution.py:52
  (4 shorter events, 0.0 us)
Async XLA Ops:
  7.2 186.9 %copy-start = (f32[1024]{0:T(1024)S(1)}, f32[1024]{0:T(1024)}, u32[]{:S(2)}) copy-start(f32[1024]{0:T(1024)} %param.14) | copy-start | bytes 12292
  7.2 33.1 %all-gather.3.cloned.1.call-start = ((), (), s32[]{:S(2)}) async-start(), calls=%async_computation.1 | async-start | bytes 1310720 | tf_op jit(solution)/shard_map/all_gather | solution.py:32
  7.9 171.6 %all-gather.5.cloned.1.call-start = ((), (), s32[]{:S(2)}) async-start(), calls=%async_computation.2 | async-start | bytes 7864320 | tf_op jit(solution)/shard_map/all_gather | solution.py:40
  40.3 16.4 %slice-start = ((s8[8388608]{0:T(1024)(128)(4,1)}), s8[4194304]{0:T(1024)(128)(4,1)S(1)}, s32[]{:S(2)}) async-start(s8[8388608]{0:T(1024)(128)(4,1)} %bitcast.19), calls=%async_computation.4 | async-start | bytes 8388608
  41.9 14.8 %slice-start.1 = ((s8[8388608]{0:T(1024)(128)(4,1)}), s8[4194304]{0:T(1024)(128)(4,1)S(1)}, s32[]{:S(2)}) async-start(s8[8388608]{0:T(1024)(128)(4,1)} %bitcast.19), calls=%async_computation.5 | async-start | bytes 8388608
  64.6 241.8 %reduce-scatter.2.cloned.1.call-start = ((), (), s32[]{:S(2)}) async-start(), calls=%async_computation.3 | async-start | bytes 18874368 | tf_op jit(solution)/shard_map/reduce_scatter | solution.py:50
  192.0 0.7 copy-start.2
  192.0 2.1 copy-start.1
  192.0 27.1 %copy-start.3 = (f32[1024]{0:T(1024)S(1)}, f32[1024]{0:T(1024)}, u32[]{:S(2)}) copy-start(f32[1024]{0:T(1024)} %param.17) | copy-start | bytes 12292
Sparse Core Ops, SparseCore 0:
  9.6 30.6 all-gather.2
  64.7 114.6 all-gather.4
  192.2 114.2 reduce-scatter.1
where the time goes:
time: 362 us; the launch traced here: 361 us
  waiting for transfers between devices  231 us (64%)
  blocking collectives  61.2 us (17%)
  matrix products  37.2 us (10%)
  between operations  17.6 us (5%)
  other arithmetic  11.5 us (3%)
    all_gather x1, waiting for transfers between devices, shards(): lax.all_gather(white, 'ind', axis=0, tiled=True)  115 us
    reduce_scatter x1, waiting for transfers between devices, shards(): lax.psum_scatter(gram_part, ('dp', 'rep'), scatter_dimension=1, tiled=True)  86 us
    psum x1, blocking collectives, shards(): trace = lax.psum(jnp.sum(covariance * gram), ('dp', 'rep', 'ind'))  39.5 us
    all_gather x1, waiting for transfers between devices, shards(): all_inducing = lax.all_gather(inducing, 'ind', axis=0, tiled=True)  30 us
    dot_general x1, matrix products, cross_cov(): inner = jnp.dot(scaled_z, scaled_x.T, precision=lax.Precision.HIGHEST)  14.8 us
    psum x1, blocking collectives, shards(): proj, fit_sum = lax.psum((local_proj, local_fit), ('dp', 'rep'))  12.9 us
    dot_general x1, matrix products, shards(): lax.dot_general(white, lax.all_gather(white, 'ind', axis=0, tiled=True),...  12.5 us
    psum x1, blocking collectives, shards(): pred_mean, sq_norm = lax.psum((mean_part, square_part), 'ind')  8.8 us
  transfers between devices with their start and end apart: 3, of which 3 were waited for; matrix products, arithmetic and copies ran while one was open for 2% of the time, Pallas kernels for 0%

commit v1 on v0

--- a/solution.py
+++ b/solution.py
@@ -2,6 +2,17 @@
 import jax.numpy as jnp
 from jax import lax
 from jax.sharding import PartitionSpec as P
+
+
+def pass_along(value, axis, along):
+    size = lax.axis_size(axis)
+    right = [(i, (i + 1) % size) for i in range(size)]
+    shards = [value]
+    for reach in range(1, size):
+        shards = [lax.ppermute(shards[0], axis, right), *shards]
+    out = jnp.concatenate(shards, axis=along)
+    shift = (lax.axis_index(axis) + 1) * shards[-1].shape[along]
+    return jnp.roll(out, shift, axis=along)
 
 
 def cross_cov(inducing, points, lengthscales, signal):
@@ -29,7 +40,7 @@
 ):
     signal = hypers[0]
     noise_var = hypers[1]
-    all_inducing = lax.all_gather(inducing, "ind", axis=0, tiled=True)
+    all_inducing = pass_along(inducing, "ind", 0)
     cross = cross_cov(all_inducing, points, lengthscales, signal)
     white = jnp.dot(whitening, cross, preferred_element_type=jnp.float32).astype(jnp.bfloat16)
     white_wide = white.astype(jnp.float32)

time: 362 us -> 356 us (0.983)
  waiting for transfers between devices: 231 us -> 223 us
    all_gather x1 -> x0, waiting for transfers between devices: 30 us -> none  [shards(): all_inducing = lax.all_gather(inducing, 'ind', axis=0, tiled=True)]
    ppermute x0 -> x3, waiting for transfers between devices: none -> 23.9 us  [pass_along(): shards = [lax.ppermute(shards[0], axis, right), *shards]]
  transfers between devices with their start and end apart: 3 -> 5, of which waited for: 3 -> 5; matrix products, arithmetic and copies ran while one was open for 2% -> 2% of each run, Pallas kernels for 0% -> 0%
where the time goes in v1:
time: 356 us; the launch traced here: 355 us
  waiting for transfers between devices  223 us (63%)
  blocking collectives  61.2 us (17%)
  matrix products  36.6 us (10%)
  between operations  18 us (5%)
  other arithmetic  10.1 us (3%)
    all_gather x1, waiting for transfers between devices, shards(): lax.all_gather(white, 'ind', axis=0, tiled=True)  113 us
    reduce_scatter x1, waiting for transfers between devices, shards(): lax.psum_scatter(gram_part, ('dp', 'rep'), scatter_dimension=1, tiled=True)  86 us
    psum x1, blocking collectives, shards(): trace = lax.psum(jnp.sum(covariance * gram), ('dp', 'rep', 'ind'))  39.5 us
    ppermute x3, waiting for transfers between devices, pass_along(): shards = [lax.ppermute(shards[0], axis, right), *shards]  23.9 us
    dot_general x1, matrix products, cross_cov(): inner = jnp.dot(scaled_z, scaled_x.T, precision=lax.Precision.HIGHEST)  13.6 us
    dot_general x1, matrix products, shards(): lax.dot_general(white, lax.all_gather(white, 'ind', axis=0, tiled=True),...  13 us
    psum x1, blocking collectives, shards(): proj, fit_sum = lax.psum((local_proj, local_fit), ('dp', 'rep'))  12.9 us
    psum x1, blocking collectives, shards(): pred_mean, sq_norm = lax.psum((mean_part, square_part), 'ind')  8.8 us
  transfers between devices with their start and end apart: 5, of which 5 were waited for; matrix products, arithmetic and copies ran while one was open for 2% of the time, Pallas kernels for 0%

profile of v1, /device:TPU:0, one launch (start us, length us, event | category | flops | bytes accessed | tf_op | source)
XLA Modules:
  0.0 355.5 jit_solution(691654738651894634)
XLA Ops:
  7.2 0.0 copy-start
  7.2 0.0 copy-start.2
  7.2 0.0 all-gather.2.cloned.1.call-start
  7.2 3.1 collective-permute-start
  10.3 8.5 %collective-permute-done = f32[1024,64]{0,1:T(8,128)S(1)} collective-permute-done((f32[1024,64]{0,1:T(8,128)}, f32[1024,64]{0,1:T(8,128)S(1)}, u32[]{:S(2)}, u32[]{:S(2)}) %collective-permute-start) | collective-permute-done | bytes 262176 | tf_op jit(solution)/shard_map/ppermute | solution.py:12
  18.9 0.0 collective-permute-start.1
  18.9 9.3 %collective-permute-done.1 = f32[1024,64]{0,1:T(8,128)S(1)} collective-permute-done((f32[1024,64]{0,1:T(8,128)S(1)}, f32[1024,64]{0,1:T(8,128)S(1)}, u32[]{:S(2)}, u32[]{:S(2)}) %collective-permute-start.1) | collective-permute-done | bytes 262176 | tf_op jit(solution)/shard_map/ppermute | solution.py:12
  28.2 0.0 collective-permute-start.2
  28.2 1.3 fusion.5
  29.5 1.0 multiply_reduce_fusion.3
  30.5 0.0 copy-start.6
  30.5 6.1 %collective-permute-done.2 = f32[1024,64]{0,1:T(8,128)S(1)} collective-permute-done((f32[1024,64]{0,1:T(8,128)S(1)}, f32[1024,64]{0,1:T(8,128)S(1)}, u32[]{:S(2)}, u32[]{:S(2)}) %collective-permute-start.2) | collective-permute-done | bytes 262176 | tf_op jit(solution)/shard_map/ppermute | solution.py:12
  36.6 0.0 copy-start.3
  36.7 1.0 constant_dynamic-update-slice_fusion.4
  37.7 0.0 copy-done.2
  37.8 0.0 copy-done.6
  37.8 0.0 slice-start
  37.8 0.2 multiply_reduce_fusion.2
  38.0 0.0 copy-done.3
  38.0 0.0 slice-start.1
  38.0 13.6 %multiply_convert_fusion = bf16[4096,768]{1,0:T(8,128)(2,1)S(1)} fusion(f32[768]{0:T(1024)S(1)} %multiply_reduce_fusion.3, f32[4096]{0:T(1024)S(1)} %multiply_reduce_fusion.2, f32[]{:T(128)} %bitcast, bf16[768,64]{0,1:T(8,128)(2,1)S(1)} %copy-done.3, f32[8192,64]{0,1:T(8,128)S(1)} %constant_dynamic-update-slice_fusion, s32[]{:T(128)S(6)} %select_n.14, ...), kind=kOutput, calls=%fused_computation | convolution fusion | flops 2435153920 | bytes 7459848 | tf_op jit(solution)/shard_map/dot_general | solution.py:23
  51.6 0.0 slice-done
  51.7 0.0 slice-done.1
  51.7 7.9 %multiply_reduce_fusion = (f32[768]{0:T(1024)S(1)}, bf16[768,1024]{1,0:T(8,128)(2,1)}) fusion(bf16[4096,768]{1,0:T(8,128)(2,1)S(1)} %multiply_convert_fusion, bf16[1024,4096]{1,0:T(8,128)(2,1)S(1)} %bitcast.20), kind=kOutput, calls=%fused_computation.1 | convolution fusion | flops 6445595648 | bytes 16256000 | tf_op jit(solution)/shard_map/dot_general | solution.py:45
  59.5 0.0 copy-start.1
  59.5 0.0 all-gather.2.cloned.1.call-update
  59.6 0.2 reduce-scatter.2.cloned.1.call-start
  59.8 113.0 %all-gather.2.cloned.1.call-done = bf16[4096,768]{0,1:T(8,128)(2,1)} async-done(((bf16[1024,768]{0,1:T(8,128)(2,1)}), bf16[4096,768]{0,1:T(8,128)(2,1)}) %all-gather.2.cloned.1.call-update) | async-done | bytes 6291472 | tf_op jit(solution)/shard_map/all_gather | solution.py:51
  172.8 0.0 copy-done.1
  172.8 13.0 %fusion.6 = f32[1024,4096]{1,0:T(8,128)} fusion(bf16[768,1024]{1,0:T(8,128)(2,1)S(1)} %copy-done.1, bf16[4096,768]{0,1:T(8,128)(2,1)} %all-gather.2.cloned.1.call-done), kind=kOutput, calls=%fused_computation.28 | convolution fusion | flops 6442450944 | bytes 24641536 | tf_op jit(solution)/shard_map/dot_general | solution.py:49
  185.9 0.0 copy-start.4
  185.9 0.0 reduce-scatter.2.cloned.1.call-update
  185.9 0.0 copy-start.5
  185.9 0.6 copy-done.4
  187.9 0.0 copy-done
  187.9 1.3 convolution_reduce_fusion
  189.3 8.8 %all-reduce.1 = (f32[768]{0:T(1024)S(1)}, f32[768]{0:T(1024)S(1)}) all-reduce(f32[768]{0:T(1024)S(1)} %get-tuple-element.11, f32[768]{0:T(1024)S(1)} %convolution_reduce_fusion), channel_id=1, replica_groups=mesh['dp'=2,'rep'=4,'ind'=4] {'ind'}, use_global_device_ids=true, to_apply=%region_6.7 | all-reduce | flops 1536 | bytes 12288 | tf_op jit(solution)/shard_map/psum | solution.py:55
  198.1 1.3 subtract_reduce_fusion
  199.4 0.7 fusion.3
  200.1 12.9 %all-reduce = (f32[1024]{0:T(1024)S(1)}, f32[]{:T(128)}) all-reduce(f32[1024]{0:T(1024)S(1)} %bitcast.18, f32[]{:T(128)} %subtract_reduce_fusion), channel_id=1, replica_groups=mesh['dp'=2,'rep'=4,'ind'=4] {'dp','rep'}, use_global_device_ids=true, to_apply=%region_3.4 | all-reduce | flops 1025 | bytes 8200 | tf_op jit(solution)/shard_map/psum | solution.py:59
  213.0 0.0 copy-done.5
  213.0 1.2 divide_add_fusion
  214.3 86.0 %reduce-scatter.2.cloned.1.call-done = f32[1024,512]{1,0:T(8,128)} async-done(((f32[1024,4096]{1,0:T(8,128)}), f32[1024,512]{1,0:T(8,128)}) %reduce-scatter.2.cloned.1.call-update) | async-done | bytes 2097168 | tf_op jit(solution)/shard_map/reduce_scatter | solution.py:61
  300.3 6.4 %multiply_reduce_fusion.1 = (f32[]{:T(128)}, f32[1024,512]{1,0:T(8,128)}) fusion(f32[1024,512]{1,0:T(8,128)} %param.15, f32[1024,512]{1,0:T(8,128)} %reduce-scatter.2.cloned.1.call-done, f32[1024,512]{1,0:T(8,128)} %param.16, f32[]{:T(128)} %bitcast.2, s32[512]{0:T(512)S(1)} %iota_add_fusion.1, s32[1024]{0:T(1024)S(1)} %iota_add_fusion), kind=kLoop, calls=%fused_computation.2 | loop fusion | flops 4194303 | bytes 8394760 | tf_op jit(solution)/shard_map/reduce_sum | solution.py:63
  306.7 39.5 %psum.39 = f32[]{:T(128)} all-reduce(f32[]{:T(128)} %get-tuple-element.7), channel_id=1, replica_groups=mesh['dp'=2,'rep'=4,'ind'=4] {'dp','rep','ind'}, use_global_device_ids=true, to_apply=%region_10.11 | all-reduce | flops 1 | bytes 8 | tf_op jit(solution)/shard_map/psum | solution.py:63
  (11 shorter events, 0.1 us)
Async XLA Ops:
  7.2 180.8 %copy-start = (f32[1024]{0:T(1024)S(1)}, f32[1024]{0:T(1024)}, u32[]{:S(2)}) copy-start(f32[1024]{0:T(1024)} %param.14) | copy-start | bytes 12292
  7.2 30.6 %copy-start.2 = (f32[1024,64]{0,1:T(8,128)S(1)}, f32[1024,64]{0,1:T(8,128)}, u32[]{:S(2)}) copy-start(f32[1024,64]{0,1:T(8,128)} %param.12) | copy-start | bytes 786436
  7.2 165.7 %all-gather.2.cloned.1.call-start = ((), (), s32[]{:S(2)}) async-start(), calls=%async_computation.1 | async-start | bytes 7864320 | tf_op jit(solution)/shard_map/all_gather | solution.py:51
  7.2 11.6 %collective-permute-start = (f32[1024,64]{0,1:T(8,128)}, f32[1024,64]{0,1:T(8,128)S(1)}, u32[]{:S(2)}, u32[]{:S(2)}) collective-permute-start(f32[1024,64]{0,1:T(8,128)} %param.12), channel_id=1, source_target_pairs={{0,1},{1,2},{2,3},{3,0},{4,5},{5,6},{6,7},{7,4},{8,9},{9,10},{10,1... | collective-permute-start | bytes 786440 | tf_op jit(solution)/shard_map/ppermute | solution.py:12
  18.9 9.3 %collective-permute-start.1 = (f32[1024,64]{0,1:T(8,128)S(1)}, f32[1024,64]{0,1:T(8,128)S(1)}, u32[]{:S(2)}, u32[]{:S(2)}) collective-permute-start(f32[1024,64]{0,1:T(8,128)S(1)} %collective-permute-done), channel_id=1, source_target_pairs={{0,1},{1,2},{2,3},{3,0},{4,5},{5,6},{6,7},{7,4},{8,9},{9,10},{10,1... | collective-permute-start | bytes 786440 | tf_op jit(solution)/shard_map/ppermute | solution.py:12
  28.2 8.4 %collective-permute-start.2 = (f32[1024,64]{0,1:T(8,128)S(1)}, f32[1024,64]{0,1:T(8,128)S(1)}, u32[]{:S(2)}, u32[]{:S(2)}) collective-permute-start(f32[1024,64]{0,1:T(8,128)S(1)} %collective-permute-done.1), channel_id=1, source_target_pairs={{0,1},{1,2},{2,3},{3,0},{4,5},{5,6},{6,7},{7,4},{8,9},{9,10},{10,1... | collective-permute-start | bytes 786440 | tf_op jit(solution)/shard_map/ppermute | solution.py:12
  30.5 7.3 %copy-start.6 = (f32[64]{0:T(128)S(1)}, f32[64]{0:T(128)}, u32[]{:S(2)}) copy-start(f32[64]{0:T(128)} %param.18) | copy-start | bytes 772
  36.6 1.4 copy-start.3
  37.8 13.9 %slice-start = ((s8[8388608]{0:T(1024)(128)(4,1)}), s8[4194304]{0:T(1024)(128)(4,1)S(1)}, s32[]{:S(2)}) async-start(s8[8388608]{0:T(1024)(128)(4,1)} %bitcast.19), calls=%async_computation.3 | async-start | bytes 8388608
  38.0 13.6 %slice-start.1 = ((s8[8388608]{0:T(1024)(128)(4,1)}), s8[4194304]{0:T(1024)(128)(4,1)S(1)}, s32[]{:S(2)}) async-start(s8[8388608]{0:T(1024)(128)(4,1)} %bitcast.19), calls=%async_computation.4 | async-start | bytes 8388608
  59.5 113.3 %copy-start.1 = (bf16[768,1024]{1,0:T(8,128)(2,1)S(1)}, bf16[768,1024]{1,0:T(8,128)(2,1)}, u32[]{:S(2)}) copy-start(bf16[768,1024]{1,0:T(8,128)(2,1)} %get-tuple-element.12) | copy-start | bytes 4718596
  59.6 240.7 %reduce-scatter.2.cloned.1.call-start = ((), (), s32[]{:S(2)}) async-start(), calls=%async_computation.2 | async-start | bytes 18874368 | tf_op jit(solution)/shard_map/reduce_scatter | solution.py:61
  185.9 0.7 copy-start.4
  185.9 27.1 %copy-start.5 = (f32[1024]{0:T(1024)S(1)}, f32[1024]{0:T(1024)}, u32[]{:S(2)}) copy-start(f32[1024]{0:T(1024)} %param.17) | copy-start | bytes 12292
Sparse Core Ops, SparseCore 0:
  59.7 113.1 all-gather.1
  186.0 114.2 reduce-scatter.1
